TPU v7x, 32 devices: a whole 2x2x4 slice. The times are simulated.
32 devices in a mesh: dp: 4 (over z), mp: 8 (over y, x, core).
Axes of the slice: x: 2, y: 2, z: 4, core: 2. Of those that a mesh axis runs over, the one named last changes fastest.
Arguments:
- inputs: bfloat16 [197, 49152], P(None, ('dp', 'mp')), may hold values from -6 to 6
- cotangent: bfloat16 [197, 49152], P(None, ('dp', 'mp')), may hold values from -1.1953125 to 1.1953125
- w_in: bfloat16 [768, 3072], P('dp', 'mp'), may hold values from -0.21875 to 0.21875
- w_out: bfloat16 [3072, 768], P('mp', 'dp'), may hold values from -0.109375 to 0.109375
- prec_in: float32 [768, 3072], P('dp', 'mp'), may hold values from 0.1 to 2
- prec_out: float32 [3072, 768], P('mp', 'dp'), may hold values from 0.1 to 2
Outputs:
- new_prec_in: float32 [768, 3072], P('dp', 'mp')
- new_prec_out: float32 [3072, 768], P('mp', 'dp')
- new_w_in: float32 [768, 3072], P('dp', 'mp')
- new_w_out: float32 [3072, 768], P('mp', 'dp')
All inputs are finite; a program needn't handle non-finite values.
Results may differ from a plain program's by a relative error of at most 0.0028.
Values may be sent and summed in bfloat16 or wider, within the bound.
A program may use at most 64 MiB of HBM per device.

v0:
```python
import jax
import jax.numpy as jnp
from jax import lax
from jax.sharding import PartitionSpec as P

D = 768
SEQ = 197


def gelu_tanh(v):
    return jax.nn.gelu(v, approximate=True)


def per_device(inputs, cotangent, w_in, w_out, prec_in, prec_out):
    w_in_full, w_out_full = (
        lax.all_gather(w_in, "dp", axis=0, tiled=True),
        lax.all_gather(w_out, "dp", axis=1, tiled=True),
    )
    whole = lax.all_gather(inputs, "mp", axis=1, tiled=True)
    rows3 = whole.reshape(SEQ, -1, D)
    images = rows3.shape[1]
    pre = jnp.einsum("snd,dh->snh", rows3, w_in_full, preferred_element_type=jnp.float32)
    act = gelu_tanh(pre).astype(jnp.bfloat16)
    cot_whole = lax.all_gather(cotangent, "mp", axis=1, tiled=True)
    cot3 = cot_whole.reshape(SEQ, images, D)
    back = jnp.einsum("snd,hd->snh", cot3, w_out_full, preferred_element_type=jnp.float32)
    per_out = jnp.einsum("snh,snd->nhd", act, cot3, preferred_element_type=jnp.float32)
    sum_out = jnp.sum(per_out, 0)
    sq_out = jnp.sum(per_out * per_out, 0)
    delta = jax.vjp(gelu_tanh, pre)[1](back)[0].astype(jnp.bfloat16)
    rows_again = lax.all_gather(inputs, "mp", axis=1, tiled=True).reshape(SEQ, images, D)
    per_in = jnp.einsum("snd,snh->ndh", rows_again, delta, preferred_element_type=jnp.float32)
    sum_in = jnp.sum(per_in, 0)
    sq_in = jnp.sum(per_in * per_in, 0)
    sum_in, sq_in = (
        lax.psum_scatter(sum_in, "dp", scatter_dimension=0, tiled=True),
        lax.psum_scatter(sq_in, "dp", scatter_dimension=0, tiled=True),
    )
    sum_out, sq_out = (
        lax.psum_scatter(sum_out, "dp", scatter_dimension=1, tiled=True),
        lax.psum_scatter(sq_out, "dp", scatter_dimension=1, tiled=True),
    )
    scale = 1.0 / (images * lax.axis_size("dp"))
    new_prec_in = 0.6 * prec_in + 0.4 * sq_in * scale
    new_prec_out = 0.6 * prec_out + 0.4 * sq_out * scale
    w_in_own = w_in.astype(jnp.float32)
    w_out_own = w_out.astype(jnp.float32)
    new_w_in = w_in_own - 1.0 * (sum_in * scale + 0.1 * w_in_own) / (new_prec_in + 0.1)
    new_w_out = w_out_own - 1.0 * (sum_out * scale + 0.1 * w_out_own) / (new_prec_out + 0.1)
    return (new_prec_in, new_prec_out, new_w_in, new_w_out)


def solution(mesh):
    placed = (
        P(None, ("dp", "mp")),
        P(None, ("dp", "mp")),
        P("dp", "mp"),
        P("mp", "dp"),
        P("dp", "mp"),
        P("mp", "dp"),
    )
    return jax.shard_map(
        per_device,
        mesh=mesh,
        in_specs=placed,
        out_specs=(P("dp", "mp"), P("mp", "dp"), P("dp", "mp"), P("mp", "dp")),
        check_vma=False,
    )
```

profile of v0, /device:TPU:0, one launch (start us, length us, event | category | flops | bytes accessed | tf_op | source)
XLA Modules:
  0.0 244.7 jit_solution(8754437066115192813)
XLA Ops:
  7.2 0.7 all-gather.5.cloned.1.call-update
  7.9 0.7 all-gather.3.cloned.1.call-update
  8.7 18.5 %all_gather.16 = bf16[768,384]{1,0:T(8,128)(2,1)S(1)} all-gather(bf16[192,384]{1,0:T(8,128)(2,1)} %param.8), channel_id=1, replica_groups=mesh['dp'=4,'mp'=8] {'dp'}, dimensions={0}, use_global_device_ids=true | all-gather | bytes 737280 | tf_op jit(solution)/shard_map/all_gather | solution.py:16
  27.2 16.3 %all_gather.14 = bf16[384,768]{0,1:T(8,128)(2,1)S(1)} all-gather(bf16[384,192]{0,1:T(8,128)(2,1)} %param.9), channel_id=1, replica_groups=mesh['dp'=4,'mp'=8] {'dp'}, dimensions={1}, use_global_device_ids=true | all-gather | bytes 737280 | tf_op jit(solution)/shard_map/all_gather | solution.py:17
  43.5 8.7 %all-gather.5.cloned.1.call-done = bf16[197,12288]{1,0:T(8,128)(2,1)} async-done(((bf16[197,1536]{1,0:T(8,128)(2,1)}), bf16[197,12288]{1,0:T(8,128)(2,1)}) %all-gather.5.cloned.1.call-update) | async-done | bytes 4841488 | tf_op jit(solution)/shard_map/all_gather | solution.py:31
  52.2 3.8 %copy.47 = bf16[25,8,16,768]{3,2,1,0:T(8,128)(2,1)S(1)} copy(bf16[25,8,16,768]{3,1,2,0:T(8,128)(2,1)} %bitcast.30) | data formatting | bytes 9830400
  56.0 2.5 %slice.1 = bf16[197,16,768]{2,1,0:T(8,128)(2,1)} slice(bf16[200,16,768]{2,1,0:T(8,128)(2,1)S(1)} %bitcast.27), slice={[0:197], [0:16], [0:768]} | slice | bytes 9682944 | tf_op jit(solution)/shard_map/reshape | solution.py:31
  58.5 5.6 %multiply_convert_fusion = (bf16[197,16,384]{2,1,0:T(8,128)(2,1)}, f32[197,16,384]{2,1,0:T(8,128)}) fusion(bf16[768,384]{1,0:T(8,128)(2,1)S(1)} %all_gather.16, bf16[200,16,768]{2,1,0:T(8,128)(2,1)S(1)} %bitcast.28), kind=kOutput, calls=%fused_computation.17 | convolution fusion | flops 1870018560 | bytes 12693504 | tf_op jit(solution)/shard_map/snd,dh->snh/dot_general | solution.py:22
  64.2 29.6 %all-gather.3.cloned.1.call-done = bf16[197,12288]{1,0:T(8,128)(2,1)} async-done(((bf16[197,1536]{1,0:T(8,128)(2,1)}), bf16[197,12288]{1,0:T(8,128)(2,1)}) %all-gather.3.cloned.1.call-update) | async-done | bytes 4841488 | tf_op jit(solution)/shard_map/all_gather | solution.py:24
  93.8 3.9 %copy.46 = bf16[25,8,16,768]{3,2,1,0:T(8,128)(2,1)S(1)} copy(bf16[25,8,16,768]{3,1,2,0:T(8,128)(2,1)} %bitcast.29) | data formatting | bytes 9830400
  97.7 2.2 copy-done
  99.9 5.4 %fusion.11 = bf16[197,16,384]{2,1,0:T(8,128)(2,1)S(1)} fusion(f32[197,16,384]{2,1,0:T(8,128)S(1)} %copy-done.5, bf16[384,768]{0,1:T(8,128)(2,1)S(1)} %all_gather.14, bf16[200,16,768]{2,1,0:T(8,128)(2,1)S(1)} %bitcast.25), kind=kOutput, calls=%fused_computation.16 | convolution fusion | flops 1883332608 | bytes 12693504 | tf_op jit(solution)/shard_map/snd,hd->snh/dot_general | solution.py:26
  105.3 8.2 %bitcast_reduce_fusion = (f32[768,384]{0,1:T(8,128)S(1)}, f32[768,384]{0,1:T(8,128)S(1)}) fusion(bf16[197,16,768]{2,1,0:T(8,128)(2,1)S(1)} %bitcast.32, bf16[197,16,384]{2,1,0:T(8,128)(2,1)S(1)} %fusion.11), kind=kOutput, calls=%fused_computation | convolution fusion | flops 1872691200 | bytes 9621504 | tf_op jit(solution)/shard_map/snd,snh->ndh/dot_general | solution.py:32
  113.5 1.4 copy.38
  115.0 1.4 copy.42
  116.7 2.8 %slice = bf16[197,16,768]{2,1,0:T(8,128)(2,1)S(1)} slice(bf16[200,16,768]{2,1,0:T(8,128)(2,1)} %bitcast.26), slice={[0:197], [0:16], [0:768]} | slice | bytes 9682944 | tf_op jit(solution)/shard_map/reshape | solution.py:25
  119.5 0.3 copy-done.6
  119.8 8.2 %fusion.23 = (f32[384,768]{1,0:T(8,128)S(1)}, f32[384,768]{1,0:T(8,128)S(1)}) fusion(bf16[197,16,768]{2,1,0:T(8,128)(2,1)S(1)} %slice, bf16[197,16,384]{2,1,0:T(8,128)(2,1)S(1)} %copy-done.6), kind=kOutput, calls=%fused_computation.35 | convolution fusion | flops 1872691200 | bytes 9621504 | tf_op jit(solution)/shard_map/snh,snd->nhd/dot_general | solution.py:27
  128.1 1.4 copy.40
  129.6 1.4 copy.44
  131.7 12.8 %reduce-scatter.13.cloned.1.call-done = f32[192,384]{1,0:T(8,128)} async-done(((f32[768,384]{1,0:T(8,128)}), f32[192,384]{1,0:T(8,128)}) %reduce-scatter.13.cloned.1.call-update) | async-done | bytes 294928
  144.5 1.1 copy.39
  145.6 29.0 %reduce-scatter.17.cloned.1.call-done = f32[192,384]{1,0:T(8,128)} async-done(((f32[768,384]{1,0:T(8,128)}), f32[192,384]{1,0:T(8,128)}) %reduce-scatter.17.cloned.1.call-update) | async-done | bytes 294928
  174.6 1.1 copy.43
  175.9 0.9 copy.34
  176.7 0.9 copy.36
  177.6 27.1 %reduce-scatter.15.cloned.1.call-done = f32[192,384]{1,0:T(8,128)} async-done(((f32[768,384]{1,0:T(8,128)}), f32[192,384]{1,0:T(8,128)}) %reduce-scatter.15.cloned.1.call-update) | async-done | bytes 294928
  204.7 1.1 copy.41
  205.8 29.0 %reduce-scatter.19.cloned.1.call-done = f32[192,384]{1,0:T(8,128)} async-done(((f32[768,384]{1,0:T(8,128)}), f32[192,384]{1,0:T(8,128)}) %reduce-scatter.19.cloned.1.call-update) | async-done | bytes 294928
  234.8 1.1 copy.45
  236.1 0.9 copy.35
  237.0 0.9 copy.37
  (33 shorter events, 1.4 us)
Async XLA Ops:
  7.2 45.1 %all-gather.5.cloned.1.call-start = ((), (), s32[]{:S(2)}) async-start(), calls=%async_computation.5 | async-start | bytes 5529600 | tf_op jit(solution)/shard_map/all_gather | solution.py:31
  7.9 85.9 %all-gather.3.cloned.1.call-start = ((), (), s32[]{:S(2)}) async-start(), calls=%async_computation.4 | async-start | bytes 5529600 | tf_op jit(solution)/shard_map/all_gather | solution.py:24
  8.6 135.8 %reduce-scatter.13.cloned.1.call-start = ((), (), s32[]{:S(2)}) async-start(), calls=%async_computation.6 | async-start | bytes 1474560
  93.8 6.1 %copy-start.5 = (f32[197,16,384]{2,1,0:T(8,128)S(1)}, f32[197,16,384]{2,1,0:T(8,128)}, u32[]{:S(2)}) copy-start(f32[197,16,384]{2,1,0:T(8,128)} %get-tuple-element.21) | copy-start | bytes 14524420
  93.8 11.5 %slice-start = ((s8[4841472]{0:T(1024)(128)(4,1)}), s8[4194304]{0:T(1024)(128)(4,1)S(1)}, s32[]{:S(2)}) async-start(s8[4841472]{0:T(1024)(128)(4,1)} %bitcast.31), calls=%async_computation.10 | async-start | bytes 8388608
  97.7 2.2 copy-start
  99.9 5.4 %slice-start.1 = ((s8[4841472]{0:T(1024)(128)(4,1)}), s8[647168]{0:T(1024)(128)(4,1)S(1)}, s32[]{:S(2)}) async-start(s8[4841472]{0:T(1024)(128)(4,1)} %bitcast.31), calls=%async_computation.11 | async-start | bytes 1294336
  115.0 59.6 %reduce-scatter.17.cloned.1.call-start = ((), (), s32[]{:S(2)}) async-start(), calls=%async_computation.8 | async-start | bytes 1474560
  116.5 88.2 %reduce-scatter.15.cloned.1.call-start = ((), (), s32[]{:S(2)}) async-start(), calls=%async_computation.7 | async-start | bytes 1474560
  116.7 3.1 %copy-start.6 = (bf16[197,16,384]{2,1,0:T(8,128)(2,1)S(1)}, bf16[197,16,384]{2,1,0:T(8,128)(2,1)}, u32[]{:S(2)}) copy-start(bf16[197,16,384]{2,1,0:T(8,128)(2,1)} %get-tuple-element.20) | copy-start | bytes 7262212
  128.0 2.9 %copy-start.1 = (bf16[192,384]{1,0:T(8,128)(2,1)S(1)}, bf16[192,384]{1,0:T(8,128)(2,1)}, u32[]{:S(2)}) copy-start(bf16[192,384]{1,0:T(8,128)(2,1)} %param.8) | copy-start | bytes 442372
  128.1 3.1 %copy-start.2 = (bf16[384,192]{0,1:T(8,128)(2,1)S(1)}, bf16[384,192]{0,1:T(8,128)(2,1)}, u32[]{:S(2)}) copy-start(bf16[384,192]{0,1:T(8,128)(2,1)} %param.9) | copy-start | bytes 442372
  128.1 3.2 %copy-start.3 = (f32[192,384]{1,0:T(8,128)S(1)}, f32[192,384]{1,0:T(8,128)}, u32[]{:S(2)}) copy-start(f32[192,384]{1,0:T(8,128)} %param.10) | copy-start | bytes 884740
  128.1 3.4 %copy-start.4 = (f32[384,192]{0,1:T(8,128)S(1)}, f32[384,192]{0,1:T(8,128)}, u32[]{:S(2)}) copy-start(f32[384,192]{0,1:T(8,128)} %param.11) | copy-start | bytes 884740
  129.5 105.3 %reduce-scatter.19.cloned.1.call-start = ((), (), s32[]{:S(2)}) async-start(), calls=%async_computation.9 | async-start | bytes 1474560
Sparse Core Ops, SparseCore 0:
  9.9 42.3 all-gather.4
  54.1 39.5 all-gather.2
  115.1 29.3 reduce-scatter.12
  146.6 27.9 reduce-scatter.16
  176.7 27.9 reduce-scatter.14
  206.9 27.9 reduce-scatter.18
where the time goes:
time: 245 us
  waiting for transfers between devices  138 us (56%)
  blocking collectives  34.8 us (14%)
  local copies, waits for them, and re-layouts  29.7 us (12%)
  matrix products  27.4 us (11%)
  between operations  14.3 us (6%)
    unnamed x10, waiting for transfers between devices  99.3 us
    all_gather x1, waiting for transfers between devices, per_device(): cot_whole = lax.all_gather(cotangent, 'mp', axis=1, tiled=True)  29.6 us
    unnamed x36, local copies, waits for them, and re-layouts  24.4 us
    all_gather x1, blocking collectives, per_device(): lax.all_gather(w_in, 'dp', axis=0, tiled=True)  18.5 us
    all_gather x1, blocking collectives, per_device(): lax.all_gather(w_out, 'dp', axis=1, tiled=True)  16.3 us
    all_gather x1, waiting for transfers between devices, per_device(): lax.all_gather(inputs, 'mp', axis=1, tiled=True).reshape(SEQ, images, D)  8.74 us
    dot_general x1, matrix products, per_device(): jnp.einsum('snh,snd->nhd', act, cot3, preferred_element_type=jnp.float32)  8.2 us
    dot_general x1, matrix products, per_device(): jnp.einsum('snd,snh->ndh', rows_again, delta, preferred_element_type=jnp....  8.2 us
  transfers between devices with their start and end apart: 6, of which 6 were waited for; matrix products, arithmetic and copies ran while one was open for 13% of the time, Pallas kernels for 0%

commit v1 on v0

--- a/solution.py
+++ b/solution.py
@@ -21,7 +21,7 @@
     images = rows3.shape[1]
     pre = jnp.einsum("snd,dh->snh", rows3, w_in_full, preferred_element_type=jnp.float32)
     act = gelu_tanh(pre).astype(jnp.bfloat16)
-    cot_whole = lax.all_gather(cotangent, "mp", axis=1, tiled=True)
+    cot_whole = jnp.concatenate(lax.all_gather(cotangent, "mp"), axis=1)
     cot3 = cot_whole.reshape(SEQ, images, D)
     back = jnp.einsum("snd,hd->snh", cot3, w_out_full, preferred_element_type=jnp.float32)
     per_out = jnp.einsum("snh,snd->nhd", act, cot3, preferred_element_type=jnp.float32)

time: 245 us -> 257 us (1.049)
  matrix products: 27.4 us -> 32.5 us
  local copies, waits for them, and re-layouts: 29.7 us -> 34.8 us
    another operation x0 -> x1, local copies, waits for them, and re-layouts: none -> 8.16 us  [per_device(): cot3 = cot_whole.reshape(SEQ, images, D)]
    unnamed x36 -> x29, local copies, waits for them, and re-layouts: 24.4 us -> 18 us
    reshape x1, local copies, waits for them, and re-layouts: 2.83 us -> 6.09 us  [per_device(): cot_whole = jnp.concatenate(lax.all_gather(cotangent, 'mp'), axis=1)]
    dot_general x1, matrix products: 5.38 us -> 8.37 us  [per_device(): jnp.einsum('snd,hd->snh', cot3, w_out_full, preferred_element_type=jnp.fl...]
where the time goes in v1:
time: 257 us; the launch traced here: 256 us
  waiting for transfers between devices  139 us (54%)
  blocking collectives  34.8 us (14%)
  local copies, waits for them, and re-layouts  34.8 us (14%)
  matrix products  32.5 us (13%)
  between operations  14.3 us (6%)
    unnamed x10, waiting for transfers between devices  101 us
    all_gather x1, waiting for transfers between devices, per_device(): cot_whole = jnp.concatenate(lax.all_gather(cotangent, 'mp'), axis=1)  29.6 us
    all_gather x1, blocking collectives, per_device(): lax.all_gather(w_in, 'dp', axis=0, tiled=True)  18.5 us
    unnamed x29, local copies, waits for them, and re-layouts  18 us
    all_gather x1, blocking collectives, per_device(): lax.all_gather(w_out, 'dp', axis=1, tiled=True)  16.3 us
    dot_general x1, matrix products, per_device(): jnp.einsum('snh,snd->nhd', act, cot3, preferred_element_type=jnp.float32)  10.1 us
    all_gather x1, waiting for transfers between devices, per_device(): lax.all_gather(inputs, 'mp', axis=1, tiled=True).reshape(SEQ, images, D)  8.74 us
    dot_general x1, matrix products, per_device(): jnp.einsum('snd,snh->ndh', rows_again, delta, preferred_element_type=jnp....  8.38 us
  transfers between devices with their start and end apart: 6, of which 6 were waited for; matrix products, arithmetic and copies ran while one was open for 13% of the time, Pallas kernels for 0%

profile of v1, /device:TPU:0, one launch (start us, length us, event | category | flops | bytes accessed | tf_op | source)
XLA Modules:
  0.0 256.0 jit_solution(14900853392925463815)
XLA Ops:
  7.2 0.7 all-gather.5.cloned.1.call-update
  7.9 0.7 all-gather.7.cloned.1.call-update
  8.7 18.5 %all_gather.20 = bf16[768,384]{1,0:T(8,128)(2,1)S(1)} all-gather(bf16[192,384]{1,0:T(8,128)(2,1)} %param.8), channel_id=1, replica_groups=mesh['dp'=4,'mp'=8] {'dp'}, dimensions={0}, use_global_device_ids=true | all-gather | bytes 737280 | tf_op jit(solution)/shard_map/all_gather | solution.py:16
  27.2 16.3 %all_gather.18 = bf16[384,768]{0,1:T(8,128)(2,1)S(1)} all-gather(bf16[384,192]{0,1:T(8,128)(2,1)} %param.9), channel_id=1, replica_groups=mesh['dp'=4,'mp'=8] {'dp'}, dimensions={1}, use_global_device_ids=true | all-gather | bytes 737280 | tf_op jit(solution)/shard_map/all_gather | solution.py:17
  43.5 8.7 %all-gather.5.cloned.1.call-done = bf16[197,12288]{1,0:T(8,128)(2,1)} async-done(((bf16[197,1536]{1,0:T(8,128)(2,1)}), bf16[197,12288]{1,0:T(8,128)(2,1)}) %all-gather.5.cloned.1.call-update) | async-done | bytes 4841488 | tf_op jit(solution)/shard_map/all_gather | solution.py:31
  52.2 3.8 %copy.49 = bf16[25,8,16,768]{3,2,1,0:T(8,128)(2,1)S(1)} copy(bf16[25,8,16,768]{3,1,2,0:T(8,128)(2,1)} %bitcast.28) | data formatting | bytes 9830400
  56.0 2.5 slice
  58.6 5.7 %multiply_convert_fusion = (bf16[197,16,384]{2,1,0:T(8,128)(2,1)}, f32[197,16,384]{2,1,0:T(8,128)}) fusion(bf16[768,384]{1,0:T(8,128)(2,1)S(1)} %all_gather.20, bf16[200,16,768]{2,1,0:T(8,128)(2,1)S(1)} %bitcast.26), kind=kOutput, calls=%fused_computation.17 | convolution fusion | flops 1870018560 | bytes 12693504 | tf_op jit(solution)/shard_map/snd,dh->snh/dot_general | solution.py:22
  64.2 29.6 %all-gather.7.cloned.1.call-done = bf16[8,197,1536]{2,1,0:T(8,128)(2,1)} async-done(((bf16[1,197,1536]{2,1,0:T(8,128)(2,1)}), bf16[8,197,1536]{2,1,0:T(8,128)(2,1)}) %all-gather.7.cloned.1.call-update) | async-done | bytes 4841488 | tf_op jit(solution)/shard_map/all_gather | solution.py:24
  93.8 6.1 %copy.29 = bf16[197,8,1536]{2,1,0:T(8,128)(2,1)} copy(bf16[197,8,1536]{2,0,1:T(8,128)(2,1)} %bitcast.27) | data formatting | bytes 9682944 | tf_op jit(solution)/shard_map/reshape | solution.py:24
  99.9 8.2 %reshape_reshape.3 = bf16[197,16,768]{2,1,0:T(8,128)(2,1)} reshape(bf16[197,8,1536]{2,1,0:T(8,128)(2,1)} %copy.29) | data formatting | bytes 9682944 | tf_op jit(solution)/shard_map/reshape;reshape | solution.py:25
  108.0 8.4 %fusion.11 = bf16[197,16,384]{2,1,0:T(8,128)(2,1)S(1)} fusion(f32[197,16,384]{2,1,0:T(8,128)} %get-tuple-element.21, bf16[197,16,768]{2,1,0:T(8,128)(2,1)} %reshape_reshape.3, bf16[384,768]{0,1:T(8,128)(2,1)S(1)} %all_gather.18), kind=kOutput, calls=%fused_computation.16 | convolution fusion | flops 1883332608 | bytes 12693504 | tf_op jit(solution)/shard_map/snd,hd->snh/dot_general | solution.py:26
  116.4 8.4 %bitcast_reduce_fusion = (f32[768,384]{0,1:T(8,128)S(1)}, f32[768,384]{0,1:T(8,128)S(1)}) fusion(bf16[197,16,768]{2,1,0:T(8,128)(2,1)S(1)} %bitcast.30, bf16[197,16,384]{2,1,0:T(8,128)(2,1)S(1)} %fusion.11), kind=kOutput, calls=%fused_computation | convolution fusion | flops 1872691200 | bytes 9621504 | tf_op jit(solution)/shard_map/snd,snh->ndh/dot_general | solution.py:32
  124.8 1.4 copy.41
  126.3 0.2 reduce-scatter.17.cloned.1.call-start
  126.5 1.4 copy.45
  128.0 10.1 %fusion.22 = (f32[384,768]{1,0:T(8,128)S(1)}, f32[384,768]{1,0:T(8,128)S(1)}) fusion(bf16[197,16,768]{2,1,0:T(8,128)(2,1)} %reshape_reshape.3, bf16[197,16,384]{2,1,0:T(8,128)(2,1)} %get-tuple-element.20), kind=kOutput, calls=%fused_computation.34 | convolution fusion | flops 1872691200 | bytes 9621504 | tf_op jit(solution)/shard_map/snh,snd->nhd/dot_general | solution.py:27
  138.1 1.4 copy.43
  139.6 1.4 copy.47
  141.3 0.2 copy.28
  141.7 14.0 %reduce-scatter.13.cloned.1.call-done = f32[192,384]{1,0:T(8,128)} async-done(((f32[768,384]{1,0:T(8,128)}), f32[192,384]{1,0:T(8,128)}) %reduce-scatter.13.cloned.1.call-update) | async-done | bytes 294928
  155.7 1.1 copy.42
  156.9 29.0 %reduce-scatter.17.cloned.1.call-done = f32[192,384]{1,0:T(8,128)} async-done(((f32[768,384]{1,0:T(8,128)}), f32[192,384]{1,0:T(8,128)}) %reduce-scatter.17.cloned.1.call-update) | async-done | bytes 294928
  185.9 1.1 copy.46
  187.2 0.9 copy.37
  188.0 0.9 copy.39
  188.9 27.1 %reduce-scatter.15.cloned.1.call-done = f32[192,384]{1,0:T(8,128)} async-done(((f32[768,384]{1,0:T(8,128)}), f32[192,384]{1,0:T(8,128)}) %reduce-scatter.15.cloned.1.call-update) | async-done | bytes 294928
  216.0 1.1 copy.44
  217.1 29.0 %reduce-scatter.19.cloned.1.call-done = f32[192,384]{1,0:T(8,128)} async-done(((f32[768,384]{1,0:T(8,128)}), f32[192,384]{1,0:T(8,128)}) %reduce-scatter.19.cloned.1.call-update) | async-done | bytes 294928
  246.1 1.1 copy.48
  247.4 0.9 copy.38
  248.3 0.9 copy.40
  (27 shorter events, 1.0 us)
Async XLA Ops:
  7.2 45.1 %all-gather.5.cloned.1.call-start = ((), (), s32[]{:S(2)}) async-start(), calls=%async_computation.4 | async-start | bytes 5529600 | tf_op jit(solution)/shard_map/all_gather | solution.py:31
  7.9 85.9 %all-gather.7.cloned.1.call-start = ((), (), s32[]{:S(2)}) async-start(), calls=%async_computation.5 | async-start | bytes 5529600 | tf_op jit(solution)/shard_map/all_gather | solution.py:24
  8.6 147.1 %reduce-scatter.13.cloned.1.call-start = ((), (), s32[]{:S(2)}) async-start(), calls=%async_computation.6 | async-start | bytes 1474560
  99.9 16.5 %slice-start = ((s8[4841472]{0:T(1024)(128)(4,1)}), s8[647168]{0:T(1024)(128)(4,1)S(1)}, s32[]{:S(2)}) async-start(s8[4841472]{0:T(1024)(128)(4,1)} %bitcast.29), calls=%async_computation.10 | async-start | bytes 1294336
  108.0 8.4 %slice-start.1 = ((s8[4841472]{0:T(1024)(128)(4,1)}), s8[4194304]{0:T(1024)(128)(4,1)S(1)}, s32[]{:S(2)}) async-start(s8[4841472]{0:T(1024)(128)(4,1)} %bitcast.29), calls=%async_computation.11 | async-start | bytes 8388608
  126.3 59.6 %reduce-scatter.17.cloned.1.call-start = ((), (), s32[]{:S(2)}) async-start(), calls=%async_computation.8 | async-start | bytes 1474560
  127.9 88.1 %reduce-scatter.15.cloned.1.call-start = ((), (), s32[]{:S(2)}) async-start(), calls=%async_computation.7 | async-start | bytes 1474560
  138.1 2.9 %copy-start = (bf16[192,384]{1,0:T(8,128)(2,1)S(1)}, bf16[192,384]{1,0:T(8,128)(2,1)}, u32[]{:S(2)}) copy-start(bf16[192,384]{1,0:T(8,128)(2,1)} %param.8) | copy-start | bytes 442372
  138.1 3.1 %copy-start.1 = (bf16[384,192]{0,1:T(8,128)(2,1)S(1)}, bf16[384,192]{0,1:T(8,128)(2,1)}, u32[]{:S(2)}) copy-start(bf16[384,192]{0,1:T(8,128)(2,1)} %param.9) | copy-start | bytes 442372
  138.1 3.2 %copy-start.2 = (f32[192,384]{1,0:T(8,128)S(1)}, f32[192,384]{1,0:T(8,128)}, u32[]{:S(2)}) copy-start(f32[192,384]{1,0:T(8,128)} %param.10) | copy-start | bytes 884740
  138.1 3.4 %copy-start.3 = (f32[384,192]{0,1:T(8,128)S(1)}, f32[384,192]{0,1:T(8,128)}, u32[]{:S(2)}) copy-start(f32[384,192]{0,1:T(8,128)} %param.11) | copy-start | bytes 884740
  139.6 106.6 %reduce-scatter.19.cloned.1.call-start = ((), (), s32[]{:S(2)}) async-start(), calls=%async_computation.9 | async-start | bytes 1474560
Sparse Core Ops, SparseCore 0:
  9.9 42.3 all-gather.4
  54.1 39.5 all-gather.6
  126.4 29.3 reduce-scatter.12
  157.9 27.9 reduce-scatter.16
  188.0 27.9 reduce-scatter.14
  218.2 27.9 reduce-scatter.18
